TPU v7x, 512 devices: a 8x2x16 block of a 8x8x16 slice. The times are simulated.
512 devices in a mesh: grp: 2 (over y), ep: 128 (over x, z), tp: 2 (over core).
Axes of the slice: x: 8, y: 2, z: 16, core: 2. Of those that a mesh axis runs over, the one named last changes fastest.
The devices are a block of a 8x8x16 slice.
Arguments:
- queries: bfloat16 [16384, 16, 576], P(('grp', 'ep'), 'tp'), parts along dimension 0, may hold values from -450 to 450
- latent_cache: bfloat16 [768, 512, 576], P(('grp', 'ep'), 'tp'), parts along dimension 0, may hold values from -6 to 6
- residual: bfloat16 [16384, 2048], P(('grp', 'ep')), parts along dimension 0, may hold values from -8 to 8
- token_request: int32 [16384], P(('grp', 'ep')), parts along dimension 0, may hold values from 0 to 2, as said below
- token_visible: int32 [16384], P(('grp', 'ep')), parts along dimension 0, may hold values from 1 to 512, as said below
- value_proj: bfloat16 [16, 512, 128], P('tp', 'ep'), may hold values from -0.25 to 0.25
- out_proj: bfloat16 [2048, 2048], P('tp', 'ep'), may hold values from -0.125 to 0.125
- norm_gain: float32 [2048], replicated, may hold values from 0.1 to 1.9
- router: bfloat16 [2048, 64], replicated, may hold values from -0.0390625 to 0.0390625
- expert_ids: int32 [16384, 6], P(('grp', 'ep')), parts along dimension 0, may hold values from 0 to 63, all different within a row; in each aligned block of 64 rows (0 to 63, 64 to 127, ...) at most 8 rows name the same one
- gate_weight: bfloat16 [128, 2048, 384], P('ep', None, 'tp'), may hold values from -0.125 to 0.125
- up_weight: bfloat16 [128, 2048, 384], P('ep', None, 'tp'), may hold values from -0.125 to 0.125
- down_weight: bfloat16 [128, 384, 2048], P('ep', 'tp'), may hold values from -0.21875 to 0.21875
Outputs:
- hidden: bfloat16 [16384, 2048], P(('grp', 'ep'), 'tp'), parts along dimension 0
- expert_out: bfloat16 [16384, 2048], P(('grp', 'ep'), 'tp'), parts along dimension 0
There are 2 independent parts, one for each index of `grp`. A program takes and returns all parts, laid end to end along the dimension named above; an argument that names none is the same for every part. Nothing has to cross between parts.
Inputs may be any that keep to these rules, and one draw needn't show every extreme that they name: `token_request`: in each ep block, 62 tokens belong to request 0, a prefill span, and each other request has exactly one token; the tokens' order in the block is arbitrary. `token_visible`: the span's tokens read consecutive counts s + 1 to s + 62; 512 is reached in every draw. `expert_ids`: each row names 6 different experts; among the 64 tokens of one ep index no expert is named by more than 8 tokens, and this bound is reached.
All inputs are finite; a program needn't handle non-finite values.
Results may differ from a plain program's by a relative error of at most 0.018.
Values may be sent and summed in bfloat16 or wider, within the bound.
A program may use at most 64 MiB of HBM per device.

v0:
```python
import jax
import jax.numpy as jnp
from jax import lax
from jax.sharding import Mesh
from jax.sharding import PartitionSpec as P

LATENT = 512
VDIM = 128
EXPERTS = 64
TOPK = 6
GROUPS = 2
CAP = 8
PIECES = 128
EP = ("ep_0", "ep_1")
GRP_EP = ("grp", "ep_0", "ep_1")


score_scale = 192.0 ** (-0.5)
epsilon = 1e-06


def from_everyone(value, axis):
    peers = lax.axis_size(axis)
    return lax.all_to_all(
        jnp.broadcast_to(value[None], (peers, *value.shape)), axis, 0, 0, tiled=True
    )


def laid_out(pieces, dim):
    lengths = list(pieces.shape[1:])
    lengths[dim] *= pieces.shape[0]
    return jnp.moveaxis(pieces, 0, dim).reshape(lengths)


def collect(value, axis, dim):
    pieces = from_everyone(value, axis)
    return laid_out(pieces, dim)


def of_everyone(value, axis):
    return from_everyone(value, axis).max(axis=0)


def split_up(value, dim, peers):
    before, after = (value.shape[:dim], value.shape[dim + 1 :])
    return jnp.moveaxis(value.reshape(*before, peers, -1, *after), dim, 0)


def sent_and_summed(value, axis, dim):
    peers = lax.axis_size(axis)
    pieces = lax.all_to_all(split_up(value, dim, peers), axis, 0, 0, tiled=True)
    return jnp.sum(pieces, axis=0)


def sent_together(arrays, axis, dim, along):
    columns = [a.reshape(*a.shape[:along], -1) for a in arrays]
    both = jnp.concatenate(columns, axis=along)
    result, at, outs = (sent_and_summed(both, axis, dim), 0, [])
    for a, column in zip(arrays, columns):
        piece = result[..., at : at + column.shape[along]]
        outs.append(piece.reshape(*piece.shape[:along], *a.shape[along:]))
        at += column.shape[along]
    return tuple(outs)


def stacked_from(value, axes, order):
    pieces = value[None]
    for k in order:
        pieces = lax.all_gather(pieces, axes[k], axis=0, tiled=True)
    carried = [lax.axis_size(axes[k]) for k in reversed(order)]
    pieces = pieces.reshape(*carried, *value.shape)
    turned = sorted(range(len(order)), key=lambda place: order[len(order) - 1 - place])
    return pieces.transpose(*turned, *range(len(order), pieces.ndim)).reshape(-1, *value.shape)


def whole_of(value, axes, order, dim):
    return laid_out(stacked_from(value, axes, order), dim)


def over_copies(value, axis):
    everything = from_everyone(value, axis)
    return jnp.sum(everything, axis=0)


def masked_scores(queries, block_rows, token_request, token_visible, offset):
    per_request = block_rows.shape[1]
    flat_rows = block_rows.reshape(-1, block_rows.shape[2])
    scores = (
        jnp.einsum("thc,kc->thk", queries, flat_rows, preferred_element_type=jnp.float32)
        * score_scale
    )
    column = jnp.arange(flat_rows.shape[0], dtype=jnp.int32)
    owner_id = column // per_request
    position = column % per_request + offset
    allowed = (owner_id[None, :] == token_request[:, None]) & (
        position[None, :] < token_visible[:, None]
    )
    return (jnp.where(allowed[:, None, :], scores, -jnp.inf), flat_rows)


def weighted_rows(scores, row_peak, flat_rows):
    weights = jnp.exp(scores - row_peak[:, :, None]).astype(jnp.bfloat16)
    totals = jnp.sum(weights.astype(jnp.float32), axis=2)
    summed = jnp.einsum(
        "thk,kc->thc", weights, flat_rows[:, :LATENT], preferred_element_type=jnp.float32
    )
    return (summed, totals)


def expert_block(arrived, gate_weight, up_weight, down_weight):
    gate_vals = jnp.einsum("prd,pdf->prf", arrived, gate_weight, preferred_element_type=jnp.float32)
    up_vals = jnp.einsum("prd,pdf->prf", arrived, up_weight, preferred_element_type=jnp.float32)
    activated = (jax.nn.silu(gate_vals) * up_vals).astype(jnp.bfloat16)
    return jnp.einsum(
        "prf,pfd->prd", activated, down_weight, preferred_element_type=jnp.float32
    ).astype(jnp.bfloat16)


def body(
    queries,
    latent_cache,
    residual,
    token_request,
    token_visible,
    value_proj,
    out_proj,
    norm_gain,
    router,
    expert_ids,
    gate_weight,
    up_weight,
    down_weight,
):
    all_heads = collect(queries, "tp", 1)
    offset = lax.axis_index("tp") * latent_cache.shape[1]
    scores, flat_rows = masked_scores(all_heads, latent_cache, token_request, token_visible, offset)
    row_peak = of_everyone(jnp.max(scores, axis=2), "tp")
    part_sum, part_total = weighted_rows(scores, row_peak, flat_rows)
    summed, totals = sent_together((part_sum, part_total), "tp", 1, 2)
    context = (summed / totals[:, :, None]).astype(jnp.bfloat16)
    tokens_here = context.shape[0]
    heads_here = context.shape[1]
    head_values = jnp.einsum(
        "thl,hlv->thv",
        context,
        whole_of(value_proj, EP, (0, 1), 1),
        preferred_element_type=jnp.float32,
    )
    heads_out = head_values.astype(jnp.bfloat16).reshape(tokens_here, heads_here * VDIM)
    attention_part = jnp.dot(
        heads_out, whole_of(out_proj, EP, (0, 1), 1), preferred_element_type=jnp.float32
    )
    attention = over_copies(attention_part, "tp")
    hidden = (residual.astype(jnp.float32) + attention).astype(jnp.bfloat16)
    hidden_wide = hidden.astype(jnp.float32)
    normed = (
        hidden_wide
        * lax.rsqrt(jnp.mean(hidden_wide * hidden_wide, axis=1, keepdims=True) + epsilon)
        * norm_gain
    ).astype(jnp.bfloat16)
    logits = jnp.dot(normed, router, preferred_element_type=jnp.float32)
    gate_share = jax.nn.softmax(jnp.take_along_axis(logits, expert_ids, axis=1), axis=1).astype(
        jnp.bfloat16
    )
    flat_ids = expert_ids.reshape(-1)
    position_id = jnp.arange(flat_ids.shape[0], dtype=jnp.int32)
    earlier = (flat_ids[:, None] == flat_ids[None, :]) & (
        position_id[None, :] < position_id[:, None]
    )
    slot_ids = (flat_ids * CAP + jnp.sum(earlier.astype(jnp.int32), axis=1)).reshape(
        tokens_here, TOPK
    )
    targets = jnp.arange(EXPERTS * CAP, dtype=jnp.int32)
    matches = slot_ids[:, :, None] == targets[None, None, :]
    picker = jnp.any(matches, axis=1).T.astype(jnp.bfloat16)
    model_width = normed.shape[1]
    mixing = jnp.sum(
        jnp.where(matches, gate_share[:, :, None], jnp.zeros((), jnp.bfloat16)), axis=1
    )
    mixing = jnp.broadcast_to(
        mixing.reshape(tokens_here, EXPERTS, 1, CAP), (tokens_here, EXPERTS, GROUPS, CAP)
    ).reshape(tokens_here, PIECES * CAP)
    core_count = lax.axis_size("tp")
    half_width = model_width // core_count
    core_start = lax.axis_index("tp") * half_width
    normed_share = lax.dynamic_slice_in_dim(normed, core_start, half_width, 1)
    outgoing = jnp.dot(picker, normed_share, preferred_element_type=jnp.float32).astype(
        jnp.bfloat16
    )
    outgoing = jnp.broadcast_to(
        outgoing.reshape(EXPERTS, 1, CAP, half_width), (EXPERTS, GROUPS, CAP, half_width)
    ).reshape(PIECES, CAP, half_width)
    arrived_share = lax.all_to_all(outgoing, EP, split_axis=0, concat_axis=1, tiled=True)
    arrived = lax.all_gather(arrived_share, "tp", axis=2, tiled=True)
    partial_out = expert_block(arrived, gate_weight, up_weight, down_weight)
    swapped = lax.all_to_all(partial_out[None], "tp", split_axis=3, concat_axis=0, tiled=True)
    returned = lax.all_to_all(swapped, EP, split_axis=2, concat_axis=1, tiled=True)
    returned = returned.reshape(core_count, PIECES * CAP, half_width)
    routed = jnp.einsum("tk,qkd->td", mixing, returned, preferred_element_type=jnp.float32)
    expert_out = routed.astype(jnp.bfloat16)
    hidden_part = lax.dynamic_slice_in_dim(hidden, core_start, half_width, 1)
    return (hidden_part, expert_out)


def solution(mesh):
    finer = Mesh(
        mesh.devices.reshape(mesh.shape["grp"], 8, 16, mesh.shape["tp"]),
        ("grp", "ep_0", "ep_1", "tp"),
    )
    in_specs = (
        P(GRP_EP, "tp", None),
        P(GRP_EP, "tp", None),
        P(GRP_EP, None),
        P(GRP_EP),
        P(GRP_EP),
        P("tp", EP, None),
        P("tp", EP),
        P(),
        P(),
        P(GRP_EP, None),
        P(EP, None, "tp"),
        P(EP, None, "tp"),
        P(EP, "tp", None),
    )
    out_specs = (P(GRP_EP, "tp"), P(GRP_EP, "tp"))
    return jax.shard_map(body, mesh=finer, in_specs=in_specs, out_specs=out_specs, check_vma=False)
```

profile of v0, /device:TPU:80, one launch (start us, length us, event | category | flops | bytes accessed | tf_op | source)
XLA Modules:
  0.0 691.2 jit_solution(127817837888464356)
XLA Ops:
  7.3 26.9 %all-gather = bf16[64,4,128]{2,1,0:T(4,128)(2,1)S(1)} all-gather(bf16[8,4,128]{2,1,0:T(4,128)(2,1)} %param.18), channel_id=2, replica_groups=mesh['grp'=2,'ep_0'=8,'ep_1'=16,'tp'=2] {'ep_0'}, dimensions={0}, use_global_device_ids=true | all-gather | bytes 73728 | tf_op jit(solution)/shard_map/all_gather | solution.py:69
  34.9 25.1 %all-gather.1 = bf16[8192,16]{0,1:T(8,128)(2,1)S(1)} all-gather(bf16[1024,16]{0,1:T(8,128)(2,1)} %param.19), channel_id=3, replica_groups=mesh['grp'=2,'ep_0'=8,'ep_1'=16,'tp'=2] {'ep_0'}, dimensions={0}, use_global_device_ids=true | all-gather | bytes 294912 | tf_op jit(solution)/shard_map/all_gather | solution.py:69
  63.2 3.7 all-to-all-start
  69.1 3.2 fusion.4
  72.5 3.7 all_to_all.59
  85.6 4.0 all-to-all-start.2
  97.2 41.3 %all-gather.6.cloned.1.call-done = bf16[128,8,4,128]{3,1,2,0:T(8,128)(2,1)} async-done(((bf16[8,8,4,128]{3,1,2,0:T(8,128)(2,1)}), bf16[128,8,4,128]{3,1,2,0:T(8,128)(2,1)}) %all-gather.6.cloned.1.call-update) | async-done | bytes 1048592 | tf_op jit(solution)/shard_map/all_gather | solution.py:69
  140.7 76.4 %all-gather.8.cloned.1.call-done = bf16[128,1024,16]{1,0,2:T(8,128)(2,1)} async-done(((bf16[8,1024,16]{1,0,2:T(8,128)(2,1)}), bf16[128,1024,16]{1,0,2:T(8,128)(2,1)}) %all-gather.8.cloned.1.call-update) | async-done | bytes 4194320 | tf_op jit(solution)/shard_map/all_gather | solution.py:69
  217.1 4.5 copy.188
  223.2 4.6 all_to_all.60
  229.0 114.0 %all_to_all.61 = bf16[128,8,1024]{2,1,0:T(8,128)(2,1)} all-to-all(bf16[128,8,1024]{2,1,0:T(8,128)(2,1)S(1)} %bitcast.107), channel_id=1, replica_groups=mesh['grp'=2,'ep_0'=8,'ep_1'=16,'tp'=2] {'ep_0','ep_1'}, dimensions={0} | all-to-all | bytes 4194304 | tf_op jit(solution)/shard_map/all_to_all | solution.py:193
  343.1 17.3 %all-gather.10.cloned.1.call-done = bf16[1,1024,2048]{2,1,0:T(8,128)(2,1)} async-done(((bf16[1,1024,1024]{2,1,0:T(8,128)(2,1)}), bf16[1,1024,2048]{2,1,0:T(8,128)(2,1)}) %all-gather.10.cloned.1.call-update) | async-done | bytes 4194320 | tf_op jit(solution)/shard_map/all_gather | solution.py:194
  360.3 4.6 fusion.2
  364.9 7.3 %convert_bitcast_fusion = bf16[1,1,1024,2048]{3,2,1,0:T(8,128)(2,1)} fusion(bf16[1,192,2048]{2,1,0:T(8,128)(2,1)S(1)} %copy-done, bf16[1,1024,2048]{2,1,0:T(8,128)(2,1)} %all-gather.10.cloned.1.call-done, bf16[1,2048,192]{1,2,0:T(8,128)(2,1)} %param.24, f32[1024,192]{0,1:T(8,128)} %fusion.2), kind=kOutput, calls=%fused_computation.6 | convolution fusion | flops 1613889536 | bytes 10747904 | tf_op jit(solution)/shard_map/prf,pfd->prd/dot_general | solution.py:114
  372.2 20.6 %copy.194 = bf16[1,1,1024,2048]{2,1,0,3:T(2,128)(2,1)} copy(bf16[1,1,1024,2048]{3,2,1,0:T(8,128)(2,1)} %convert_bitcast_fusion) | data formatting | bytes 8388608 | tf_op jit(solution)/shard_map/broadcast_in_dim | solution.py:196
  393.3 26.0 %reduce.4 = bf16[2048,1024]{1,0:T(8,128)(2,1)} reduce(bf16[2048,1,1,1024]{3,2,1,0:T(2,128)(2,1)} %bitcast.102, bf16[]{:T(256)} %broadcast.147), dimensions={1,2}, to_apply=%bitcast.85.reduce_sub_computation | reduce | bytes 8388610
  419.3 5.9 reshape.241
  425.2 11.9 %all_to_all.62 = bf16[2,2,524288]{2,1,0:T(2,128)(2,1)} all-to-all(bf16[2,2,524288]{2,1,0:T(2,128)(2,1)} %reshape.241), channel_id=1, replica_groups=mesh['grp'=2,'ep_0'=8,'ep_1'=16,'tp'=2] {'tp'}, dimensions={0} | all-to-all | bytes 8388608 | tf_op jit(solution)/shard_map/all_to_all | solution.py:196
  437.1 7.1 %reshape.242 = bf16[2048,1,1,1024]{3,2,1,0:T(2,128)(2,1)} reshape(bf16[2,2,524288]{2,1,0:T(2,128)(2,1)} %all_to_all.62) | data formatting | bytes 8388608
  444.2 7.1 %copy.200 = bf16[1,1,1024,2048]{2,3,0,1:T(8,128)(2,1)} copy(bf16[1,1,1024,2048]{2,1,0,3:T(2,128)(2,1)} %bitcast.103) | data formatting | bytes 8388608
  451.2 11.3 %copy.195 = bf16[2,1,1024,1024]{3,0,1,2:T(2,128)(2,1)} copy(bf16[2,1,1024,1024]{2,3,0,1:T(8,128)(2,1)} %bitcast.104) | data formatting | bytes 8388608 | tf_op jit(solution)/shard_map/all_to_all | solution.py:196
  462.5 23.8 %all-to-all-start.6 = ((bf16[2,1,1024,1024]{3,0,1,2:T(2,128)(2,1)}), bf16[2,1,1024,1024]{3,0,1,2:T(2,128)(2,1)}, u32[]{:S(2)}, u32[]{:S(2)}) async-start(bf16[2,1,1024,1024]{3,0,1,2:T(2,128)(2,1)} %copy.195), calls=%async_computation.6 | async-start | bytes 8388608 | tf_op jit(solution)/shard_map/all_to_all | solution.py:197
  491.0 179.9 %all-to-all-done.6 = bf16[2,1,1024,1024]{3,0,1,2:T(2,128)(2,1)} async-done(((bf16[2,1,1024,1024]{3,0,1,2:T(2,128)(2,1)}), bf16[2,1,1024,1024]{3,0,1,2:T(2,128)(2,1)}, u32[]{:S(2)}, u32[]{:S(2)}) %all-to-all-start.6) | async-done | bytes 4194336 | tf_op jit(solution)/shard_map/all_to_all | solution.py:197
  670.9 12.4 %convert_reduce_fusion = bf16[1024,1024]{1,0:T(8,128)(2,1)S(1)} fusion(bf16[2,1,1024,1024]{3,0,1,2:T(2,128)(2,1)} %all-to-all-done.6), kind=kLoop, calls=%fused_computation.1 | loop fusion | flops 3145728 | bytes 6291456 | tf_op jit(solution)/shard_map/tk,qkd->td/reduce_sum | solution.py:199
  (82 shorter events, 34.6 us)
Async XLA Ops:
  7.2 357.7 %copy-start = (bf16[1,192,2048]{2,1,0:T(8,128)(2,1)S(1)}, bf16[1,192,2048]{2,1,0:T(8,128)(2,1)}, u32[]{:S(2)}) copy-start(bf16[1,192,2048]{2,1,0:T(8,128)(2,1)} %param.25) | copy-start | bytes 2359300
  7.2 131.3 %all-gather.6.cloned.1.call-start = ((), (), s32[]{:S(2)}) async-start(), calls=%async_computation.7 | async-start | bytes 1114112 | tf_op jit(solution)/shard_map/all_gather | solution.py:69
  34.8 182.3 %all-gather.8.cloned.1.call-start = ((), (), s32[]{:S(2)}) async-start(), calls=%async_computation.8 | async-start | bytes 4456448 | tf_op jit(solution)/shard_map/all_gather | solution.py:69
  60.9 7.5 %copy-start.6 = (s32[64]{0:T(128)S(1)}, s32[64]{0:T(128)}, u32[]{:S(2)}) copy-start(s32[64]{0:T(128)} %param.17) | copy-start | bytes 772
  60.9 7.5 %copy-start.7 = (s32[64]{0:T(128)S(1)}, s32[64]{0:T(128)}, u32[]{:S(2)}) copy-start(s32[64]{0:T(128)} %param.16) | copy-start | bytes 772
  63.2 5.9 all-to-all-start
  85.6 4.6 copy-start.4
  85.6 7.2 %all-to-all-start.2 = ((f32[2,64,8,513]{3,2,1,0:T(8,128)}), f32[2,64,8,513]{3,2,1,0:T(8,128)S(1)}, u32[]{:S(2)}, u32[]{:S(2)}) async-start(f32[2,64,8,513]{3,2,1,0:T(8,128)} %maximum_bitcast_fusion), calls=%async_computation.2 | async-start | bytes 5242880 | tf_op jit(solution)/shard_map/all_to_all | solution.py:51
  89.7 270.6 %all-gather.10.cloned.1.call-start = ((), (), s32[]{:S(2)}) async-start(), calls=%async_computation.9 | async-start | bytes 6291456 | tf_op jit(solution)/shard_map/all_gather | solution.py:194
  223.0 4.8 copy-start.3
  223.1 5.0 copy-start.5
  229.0 131.3 %copy-start.8 = (bf16[1,2048,192]{1,2,0:T(8,128)(2,1)S(1)}, bf16[1,2048,192]{1,2,0:T(8,128)(2,1)}, u32[]{:S(2)}) copy-start(bf16[1,2048,192]{1,2,0:T(8,128)(2,1)} %param.23) | copy-start | bytes 2359300
  462.5 24.1 %copy-start.2 = (bf16[2048,64]{0,1:T(8,128)(2,1)S(1)}, bf16[2048,64]{0,1:T(8,128)(2,1)}, u32[]{:S(2)}) copy-start(bf16[2048,64]{0,1:T(8,128)(2,1)} %param.21) | copy-start | bytes 786436
  462.5 208.3 %all-to-all-start.6 = ((bf16[2,1,1024,1024]{3,0,1,2:T(2,128)(2,1)}), bf16[2,1,1024,1024]{3,0,1,2:T(2,128)(2,1)}, u32[]{:S(2)}, u32[]{:S(2)}) async-start(bf16[2,1,1024,1024]{3,0,1,2:T(2,128)(2,1)} %copy.195), calls=%async_computation.6 | async-start | bytes 8388608 | tf_op jit(solution)/shard_map/all_to_all | solution.py:197
  490.3 194.2 %copy-start.1 = (bf16[1,192,2048]{2,1,0:T(8,128)(2,1)S(1)}, bf16[1,192,2048]{2,1,0:T(8,128)(2,1)}, u32[]{:S(2)}) copy-start(bf16[1,192,2048]{2,1,0:T(8,128)(2,1)} %param.25) | copy-start | bytes 2359300
Sparse Core Ops, SparseCore 0:
  34.9 103.4 all-gather.5
  140.6 76.5 all-gather.7
  343.2 17.0 all-gather.9
where the time goes:
time: 699 us; the launch traced here: 691 us
  waiting for transfers between devices  318 us (45%)
  blocking collectives  186 us (27%)
  local copies, waits for them, and re-layouts  71.6 us (10%)
  other arithmetic  47.6 us (7%)
  starting transfers between devices  32.1 us (5%)
  matrix products  21.9 us (3%)
  between operations  14.3 us (2%)
    all_to_all x1, waiting for transfers between devices, body(): lax.all_to_all(swapped, EP, split_axis=2, concat_axis=1, tiled=True)  180 us
    all_gather x2, waiting for transfers between devices, stacked_from(): pieces = lax.all_gather(pieces, axes[k], axis=0, tiled=True)  118 us
    all_to_all x1, blocking collectives, body(): lax.all_to_all(outgoing, EP, split_axis=0, concat_axis=1, tiled=True)  114 us
    all_gather x2, blocking collectives, stacked_from(): pieces = lax.all_gather(pieces, axes[k], axis=0, tiled=True)  52 us
    unnamed x1, other arithmetic  26 us
    all_to_all x1, starting transfers between devices, body(): lax.all_to_all(swapped, EP, split_axis=2, concat_axis=1, tiled=True)  23.8 us
    unnamed x28, local copies, waits for them, and re-layouts  23.3 us
    broadcast_in_dim x1, local copies, waits for them, and re-layouts, body(): partial_out[None]  20.6 us
  transfers between devices with their start and end apart: 6, of which 6 were waited for; matrix products, arithmetic and copies ran while one was open for 4% of the time, Pallas kernels for 0%

commit v1 on v0

--- a/solution.py
+++ b/solution.py
@@ -1,6 +1,8 @@
 import jax
 import jax.numpy as jnp
 from jax import lax
+from jax.experimental import pallas as pl
+from jax.experimental.pallas import tpu as pltpu
 from jax.sharding import Mesh
 from jax.sharding import PartitionSpec as P
 
@@ -11,6 +13,7 @@
 GROUPS = 2
 CAP = 8
 PIECES = 128
+MESH = pl.DeviceIdType.MESH
 EP = ("ep_0", "ep_1")
 GRP_EP = ("grp", "ep_0", "ep_1")
 
@@ -107,13 +110,288 @@
     return (summed, totals)
 
 
-def expert_block(arrived, gate_weight, up_weight, down_weight):
-    gate_vals = jnp.einsum("prd,pdf->prf", arrived, gate_weight, preferred_element_type=jnp.float32)
-    up_vals = jnp.einsum("prd,pdf->prf", arrived, up_weight, preferred_element_type=jnp.float32)
-    activated = (jax.nn.silu(gate_vals) * up_vals).astype(jnp.bfloat16)
-    return jnp.einsum(
-        "prf,pfd->prd", activated, down_weight, preferred_element_type=jnp.float32
-    ).astype(jnp.bfloat16)
+def ring_ids(axis):
+    size = lax.axis_size(axis)
+    me = lax.axis_index(axis)
+    return me, lax.rem(me + 1, size), lax.rem(me + size - 1, size), size
+
+
+def wait_bytes(view, sem):
+    pltpu.make_async_copy(view, view, sem).wait()
+
+
+def moe_kernel(
+    meta_ref, tok_ref, gate_ref, up_ref, down_ref, out_ref,
+    blk, met, mix, picked, rows, rowsx, act, actx, downx, outs, ret, rss, rsl, rsr,
+    ag_s, ag_r, am_s, am_r, x_s, x_r, d_s, d_r, a_s, a_r, w_s, w_r, t_s, t_r, rs_s, rs_r,
+):
+    x, _, _, nx = ring_ids("ep_0")
+    z, right, left, nz = ring_ids("ep_1")
+    core = lax.axis_index("tp")
+    other = 1 - core
+    steps = nz // 2
+    toks, half = tok_ref.shape
+    rows_n = nx * 2 * CAP
+
+    barrier = pltpu.get_barrier_semaphore()
+    for name, peer in (("ep_1", left), ("ep_1", right), ("tp", other)):
+        pl.semaphore_signal(barrier, inc=1, device_id={name: peer}, device_id_type=MESH)
+    for j in range(1, nx):
+        pl.semaphore_signal(
+            barrier, inc=1, device_id={"ep_0": lax.rem(x + j, nx)}, device_id_type=MESH
+        )
+    pl.semaphore_wait(barrier, 3 + nx - 1)
+
+    def remote(src, dst, ssem, rsem, axis, peer):
+        return pltpu.make_async_remote_copy(
+            src_ref=src, dst_ref=dst, send_sem=ssem, recv_sem=rsem,
+            device_id={axis: peer}, device_id_type=MESH,
+        )
+
+    def gather_copy(src, slot, side, what):
+        ssem, rsem = (ag_s, ag_r) if what is blk else (am_s, am_r)
+        peer = right if side == 0 else left
+        return remote(
+            src, what.at[slot, side], ssem.at[slot, side], rsem.at[slot, side], "ep_1", peer
+        )
+
+    for side, slot in ((0, 0), (1, 1)):
+        gather_copy(meta_ref, slot, side, met).start()
+        gather_copy(tok_ref, slot, side, blk).start()
+    mine = pl.ds(pl.multiple_of(core * half, half), half)
+    theirs = pl.ds(pl.multiple_of(other * half, half), half)
+    swap = remote(down_ref.at[:, theirs], downx, w_s, w_r, "tp", other)
+    swap.start()
+    blk[0, 1] = tok_ref[...]
+    met[0, 1] = meta_ref[...]
+
+    row = lax.broadcasted_iota(jnp.int32, (rows_n, 2 * toks), 0)
+    lane = lax.broadcasted_iota(jnp.int32, (rows_n, 2 * toks), 1)
+    side_of_row = (row // CAP) % 2
+    expert = (row // (2 * CAP)) * (nz // 2) + z // 2
+    want = jnp.where(side_of_row == lane // toks, expert * CAP + row % CAP, -1).astype(jnp.float32)
+    first_half = lax.broadcasted_iota(jnp.int32, (16, 2 * toks), 1) < toks
+
+    def pick(g):
+        both = jnp.where(first_half, met[g, 0], met[g, 1])
+        share = jnp.zeros((rows_n, 2 * toks), jnp.float32)
+        chosen = jnp.zeros((rows_n, 2 * toks), jnp.float32)
+        for k in range(TOPK):
+            same = want == both[k : k + 1, :]
+            share = share + jnp.where(same, both[8 + k : 9 + k, :], 0.0)
+            chosen = chosen + jnp.where(same, 1.0, 0.0)
+        mix[g] = share.T.astype(jnp.bfloat16)
+        tokens = blk[g].reshape(2 * toks, half)
+        got = jnp.dot(chosen.astype(jnp.bfloat16), tokens, preferred_element_type=jnp.float32)
+        picked[g] = got.astype(jnp.bfloat16).reshape(nx, 2 * CAP, half)
+        rows[g, x] = picked[g, x]
+        for j in range(1, nx):
+            peer = lax.rem(x + j, nx)
+            remote(picked.at[g, peer], rows.at[g, x], x_s.at[g], x_r.at[g], "ep_0", peer).start()
+
+    def stage_gather(g):
+        gather_copy(met.at[0, 0], g, 0, met).wait_recv()
+        gather_copy(blk.at[0, 0], g, 0, blk).wait_recv()
+
+        @pl.when(g > 0)
+        def _():
+            gather_copy(met.at[0, 0], g, 1, met).wait_recv()
+            gather_copy(blk.at[0, 0], g, 1, blk).wait_recv()
+
+        @pl.when(g < steps - 1)
+        def _():
+            gather_copy(met.at[g, 0], g + 1, 0, met).start()
+            gather_copy(blk.at[g, 0], g + 1, 0, blk).start()
+
+        @pl.when((g > 0) & (g < steps - 1))
+        def _():
+            gather_copy(met.at[g, 1], g + 1, 1, met).start()
+            gather_copy(blk.at[g, 1], g + 1, 1, blk).start()
+
+        pick(g)
+
+    def rows_swap(g):
+        return remote(rows.at[g], rowsx.at[g], d_s.at[g], d_r.at[g], "tp", other)
+
+    def act_swap(g):
+        return remote(act.at[g], actx.at[g], a_s.at[g], a_r.at[g], "tp", other)
+
+    def stage_arrive(g):
+        wait_bytes(rows.at[g, pl.ds(0, nx - 1)], x_r.at[g])
+        rows_swap(g).start()
+
+    def stage_up(g):
+        rows_swap(g).wait_recv()
+        here = rows[g].reshape(rows_n, half)
+        there = rowsx[g].reshape(rows_n, half)
+
+        def into(weight):
+            return jnp.dot(here, weight[mine, :], preferred_element_type=jnp.float32) + jnp.dot(
+                there, weight[theirs, :], preferred_element_type=jnp.float32
+            )
+
+        gate_vals = into(gate_ref)
+        up_vals = into(up_ref)
+        act[g] = (gate_vals / (1.0 + jnp.exp(-gate_vals)) * up_vals).astype(jnp.bfloat16)
+        act_swap(g).start()
+
+    def stage_down(g):
+        act_swap(g).wait_recv()
+        total = jnp.dot(act[g], down_ref[:, mine], preferred_element_type=jnp.float32)
+        total = total + jnp.dot(actx[g], downx[...], preferred_element_type=jnp.float32)
+        outs[g] = total.astype(jnp.bfloat16).reshape(nx, 2 * CAP, half)
+
+    def tick(t, carry):
+        @pl.when(t < steps)
+        def _():
+            stage_gather(t)
+
+        @pl.when((t >= 1) & (t < steps + 1))
+        def _():
+            stage_arrive(t - 1)
+
+        @pl.when((t >= 2) & (t < steps + 2))
+        def _():
+            stage_up(t - 2)
+
+        @pl.when(t >= 3)
+        def _():
+            stage_down(t - 3)
+
+        return carry
+
+    swap.wait_recv()
+    lax.fori_loop(0, steps + 3, tick, 0)
+
+    def send_back(i, carry):
+        g = steps - 1 - i
+        ret[g, x] = outs[g, x]
+        for j in range(1, nx):
+            peer = lax.rem(x + j, nx)
+            remote(outs.at[g, peer], ret.at[g, x], t_s.at[g], t_r.at[g], "ep_0", peer).start()
+        return carry
+
+    lax.fori_loop(0, steps, send_back, 0)
+
+    def left_copy(g):
+        return remote(rss.at[g, 0], rsl.at[g], rs_s.at[g, 0], rs_r.at[g, 0], "ep_1", left)
+
+    def right_copy(g):
+        return remote(rss.at[g, 1], rsr.at[g], rs_s.at[g, 1], rs_r.at[g, 1], "ep_1", right)
+
+    def mixed(g):
+        wait_bytes(ret.at[g, pl.ds(0, nx - 1)], t_r.at[g])
+        return jnp.dot(
+            mix[g], ret[g].reshape(rows_n, half), preferred_element_type=jnp.float32
+        )
+
+    def combine(i, carry):
+        g = steps - 1 - i
+        part = mixed(g)
+
+        @pl.when(i == 0)
+        def _():
+            rss[g, 0] = part[:toks].astype(jnp.bfloat16)
+            rss[g, 1] = part[toks:].astype(jnp.bfloat16)
+
+        @pl.when(i > 0)
+        def _():
+            left_copy(g + 1).wait_recv()
+            right_copy(g + 1).wait_recv()
+            rss[g, 0] = (part[:toks] + rsl[g + 1].astype(jnp.float32)).astype(jnp.bfloat16)
+            rss[g, 1] = (part[toks:] + rsr[g + 1].astype(jnp.float32)).astype(jnp.bfloat16)
+
+        left_copy(g).start()
+        right_copy(g).start()
+        return carry
+
+    lax.fori_loop(0, steps - 1, combine, 0)
+    part = mixed(0)
+    left_copy(1).wait_recv()
+    right_copy(1).wait_recv()
+    rss[0, 0] = (part[:toks] + rsl[1].astype(jnp.float32)).astype(jnp.bfloat16)
+    left_copy(0).start()
+    total = part[toks:] + rsr[1].astype(jnp.float32)
+    left_copy(0).wait_recv()
+    out_ref[...] = (total + rsl[0].astype(jnp.float32)).astype(jnp.bfloat16)
+
+    swap.wait_send()
+
+    def drain(g, carry):
+        wait_bytes(picked.at[g, pl.ds(0, nx - 1)], x_s.at[g])
+        wait_bytes(outs.at[g, pl.ds(0, nx - 1)], t_s.at[g])
+        rows_swap(g).wait_send()
+        act_swap(g).wait_send()
+        gather_copy(met.at[0, 0], g, 0, met).wait_send()
+        gather_copy(blk.at[0, 0], g, 0, blk).wait_send()
+        left_copy(g).wait_send()
+
+        @pl.when(g > 0)
+        def _():
+            gather_copy(met.at[0, 0], g, 1, met).wait_send()
+            gather_copy(blk.at[0, 0], g, 1, blk).wait_send()
+            right_copy(g).wait_send()
+
+        return carry
+
+    lax.fori_loop(0, steps, drain, 0)
+
+
+def routed_experts(meta, tokens, gate_weight, up_weight, down_weight):
+    toks, half = tokens.shape
+    nx, nz = lax.axis_size("ep_0"), lax.axis_size("ep_1")
+    steps, hidden = nz // 2, gate_weight.shape[1]
+    rows_n = nx * 2 * CAP
+    bf = jnp.bfloat16
+    group = (steps, nx, 2 * CAP, half)
+    dma = pltpu.SemaphoreType.DMA
+    return pl.pallas_call(
+        moe_kernel,
+        out_shape=jax.ShapeDtypeStruct((toks, half), bf),
+        in_specs=[pl.BlockSpec(memory_space=pltpu.VMEM)] * 5,
+        out_specs=pl.BlockSpec(memory_space=pltpu.VMEM),
+        scratch_shapes=[
+            pltpu.VMEM((steps, 2, toks, half), bf),
+            pltpu.VMEM((steps, 2, 16, 2 * toks), jnp.float32),
+            pltpu.VMEM((steps, 2 * toks, rows_n), bf),
+            pltpu.VMEM(group, bf),
+            pltpu.VMEM(group, bf),
+            pltpu.VMEM(group, bf),
+            pltpu.VMEM((steps, rows_n, hidden), bf),
+            pltpu.VMEM((steps, rows_n, hidden), bf),
+            pltpu.VMEM((hidden, half), bf),
+            pltpu.VMEM(group, bf),
+            pltpu.VMEM(group, bf),
+            pltpu.VMEM((steps, 2, toks, half), bf),
+            pltpu.VMEM((steps, toks, half), bf),
+            pltpu.VMEM((steps, toks, half), bf),
+            dma((steps, 2)), dma((steps, 2)), dma((steps, 2)), dma((steps, 2)),
+            dma((steps,)), dma((steps,)), dma((steps,)), dma((steps,)),
+            dma((steps,)), dma((steps,)), dma, dma,
+            dma((steps,)), dma((steps,)), dma((steps, 2)), dma((steps, 2)),
+        ],
+        compiler_params=pltpu.CompilerParams(
+            collective_id=1, has_side_effects=True, vmem_limit_bytes=60 * 2**20
+        ),
+        name="routed_experts",
+    )(meta, tokens, gate_weight, up_weight, down_weight)
+
+
+def routing_table(logits, expert_ids):
+    tokens, top = expert_ids.shape
+    experts = jnp.arange(logits.shape[1], dtype=jnp.int32)
+    named = expert_ids[:, :, None] == experts[None, None, :]
+    chosen = jnp.sum(jnp.where(named, logits[:, None, :], 0.0), axis=2)
+    gate_share = jax.nn.softmax(chosen, axis=1).astype(jnp.bfloat16).astype(jnp.float32)
+    counts = jnp.sum(named.astype(jnp.float32), axis=1)
+    token = jnp.arange(tokens, dtype=jnp.int32)
+    before = (token[None, :] < token[:, None]).astype(jnp.float32)
+    earlier = jnp.dot(before, counts, preferred_element_type=jnp.float32)
+    place = jnp.sum(jnp.where(named, earlier[:, None, :], 0.0), axis=2)
+    slot = expert_ids.astype(jnp.float32) * CAP + place
+    fill = jnp.zeros((tokens, 8 - top), jnp.float32)
+    table = jnp.concatenate([slot, fill - 2.0, gate_share, fill], axis=1).T
+    return jnp.concatenate([table, table], axis=1)
 
 
 def body(
@@ -159,45 +437,13 @@
         * norm_gain
     ).astype(jnp.bfloat16)
     logits = jnp.dot(normed, router, preferred_element_type=jnp.float32)
-    gate_share = jax.nn.softmax(jnp.take_along_axis(logits, expert_ids, axis=1), axis=1).astype(
-        jnp.bfloat16
-    )
-    flat_ids = expert_ids.reshape(-1)
-    position_id = jnp.arange(flat_ids.shape[0], dtype=jnp.int32)
-    earlier = (flat_ids[:, None] == flat_ids[None, :]) & (
-        position_id[None, :] < position_id[:, None]
-    )
-    slot_ids = (flat_ids * CAP + jnp.sum(earlier.astype(jnp.int32), axis=1)).reshape(
-        tokens_here, TOPK
-    )
-    targets = jnp.arange(EXPERTS * CAP, dtype=jnp.int32)
-    matches = slot_ids[:, :, None] == targets[None, None, :]
-    picker = jnp.any(matches, axis=1).T.astype(jnp.bfloat16)
-    model_width = normed.shape[1]
-    mixing = jnp.sum(
-        jnp.where(matches, gate_share[:, :, None], jnp.zeros((), jnp.bfloat16)), axis=1
-    )
-    mixing = jnp.broadcast_to(
-        mixing.reshape(tokens_here, EXPERTS, 1, CAP), (tokens_here, EXPERTS, GROUPS, CAP)
-    ).reshape(tokens_here, PIECES * CAP)
-    core_count = lax.axis_size("tp")
-    half_width = model_width // core_count
+    meta = routing_table(logits, expert_ids)
+    half_width = normed.shape[1] // lax.axis_size("tp")
     core_start = lax.axis_index("tp") * half_width
     normed_share = lax.dynamic_slice_in_dim(normed, core_start, half_width, 1)
-    outgoing = jnp.dot(picker, normed_share, preferred_element_type=jnp.float32).astype(
-        jnp.bfloat16
-    )
-    outgoing = jnp.broadcast_to(
-        outgoing.reshape(EXPERTS, 1, CAP, half_width), (EXPERTS, GROUPS, CAP, half_width)
-    ).reshape(PIECES, CAP, half_width)
-    arrived_share = lax.all_to_all(outgoing, EP, split_axis=0, concat_axis=1, tiled=True)
-    arrived = lax.all_gather(arrived_share, "tp", axis=2, tiled=True)
-    partial_out = expert_block(arrived, gate_weight, up_weight, down_weight)
-    swapped = lax.all_to_all(partial_out[None], "tp", split_axis=3, concat_axis=0, tiled=True)
-    returned = lax.all_to_all(swapped, EP, split_axis=2, concat_axis=1, tiled=True)
-    returned = returned.reshape(core_count, PIECES * CAP, half_width)
-    routed = jnp.einsum("tk,qkd->td", mixing, returned, preferred_element_type=jnp.float32)
-    expert_out = routed.astype(jnp.bfloat16)
+    expert_out = routed_experts(
+        meta, normed_share, gate_weight[0], up_weight[0], down_weight[0]
+    )
     hidden_part = lax.dynamic_slice_in_dim(hidden, core_start, half_width, 1)
     return (hidden_part, expert_out)
 

time: 699 us -> 360 us (0.52)
  waiting for transfers between devices: 318 us -> 119 us
  Pallas kernels: 0 us -> 120 us
  blocking collectives: 186 us -> 66.1 us
  local copies, waits for them, and re-layouts: 71.6 us -> 22.8 us
  other arithmetic: 47.6 us -> 5.18 us
  starting transfers between devices: 32.1 us -> 3.78 us
  matrix products: 21.9 us -> 7.74 us
    all_to_all x2 -> x0, waiting for transfers between devices: 182 us -> none  [the longest x1 180 us: body(): lax.all_to_all(swapped, EP, split_axis=2, concat_axis=1, tiled=True)]
    all_to_all x2 -> x1, blocking collectives: 126 us -> 5.86 us  [sent_and_summed(): pieces = lax.all_to_all(split_up(value, dim, peers), axis, 0, 0, tiled=True)]
    pallas_call x0 -> x1, Pallas kernels: none -> 120 us  [routed_experts(): pl.pallas_call(moe_kernel, out_shape=jax.ShapeDtypeStruct((toks, half), b...]
    all_to_all x2 -> x0, starting transfers between devices: 27.8 us -> none  [the longest x1 23.8 us: body(): lax.all_to_all(swapped, EP, split_axis=2, concat_axis=1, tiled=True)]
    unnamed x1 -> x0, other arithmetic: 26 us -> none
    broadcast_in_dim x3 -> x1, local copies, waits for them, and re-layouts: 20.9 us -> 0.01 us  [routing_table(): fill = jnp.zeros((tokens, 8 - top), jnp.float32)]
    all_gather x1 -> x0, waiting for transfers between devices: 17.3 us -> none  [body(): arrived = lax.all_gather(arrived_share, 'tp', axis=2, tiled=True)]
    unnamed x28 -> x30, local copies, waits for them, and re-layouts: 23.3 us -> 8.65 us
  transfers between devices with their start and end apart: 6 -> 3, of which waited for: 6 -> 3; matrix products, arithmetic and copies ran while one was open for 4% -> 6% of each run, Pallas kernels for 0% -> 0%
where the time goes in v1:
time: 360 us; the launch traced here: 359 us
  Pallas kernels  120 us (33%)
  waiting for transfers between devices  119 us (33%)
  blocking collectives  66.1 us (18%)
  local copies, waits for them, and re-layouts  22.8 us (6%)
  between operations  14.3 us (4%)
  matrix products  7.74 us (2%)
  other arithmetic  5.18 us (1%)
  starting transfers between devices  3.78 us (1%)
    pallas_call x1, Pallas kernels, routed_experts(): pl.pallas_call(moe_kernel, out_shape=jax.ShapeDtypeStruct((toks, half), b...  120 us
    all_gather x2, waiting for transfers between devices, stacked_from(): pieces = lax.all_gather(pieces, axes[k], axis=0, tiled=True)  119 us
    all_gather x2, blocking collectives, stacked_from(): pieces = lax.all_gather(pieces, axes[k], axis=0, tiled=True)  52 us
    unnamed x30, local copies, waits for them, and re-layouts  8.65 us
    all_to_all x2, blocking collectives, from_everyone(): lax.all_to_all(jnp.broadcast_to(value[None], (peers, *value.shape)), axis...  8.32 us
  transfers between devices with their start and end apart: 3, of which 3 were waited for; matrix products, arithmetic and copies ran while one was open for 6% of the time, Pallas kernels for 0%

profile of v1, /device:TPU:80, one launch (start us, length us, event | category | flops | bytes accessed | tf_op | source)
XLA Modules:
  0.0 359.2 jit_solution(1405792265094276498)
XLA Ops:
  7.3 26.9 %all-gather = bf16[64,4,128]{2,1,0:T(4,128)(2,1)S(1)} all-gather(bf16[8,4,128]{2,1,0:T(4,128)(2,1)} %param.18), channel_id=2, replica_groups=mesh['grp'=2,'ep_0'=8,'ep_1'=16,'tp'=2] {'ep_0'}, dimensions={0}, use_global_device_ids=true | all-gather | bytes 73728 | tf_op jit(solution)/shard_map/all_gather | solution.py:72
  34.9 25.1 %all-gather.1 = bf16[8192,16]{0,1:T(8,128)(2,1)S(1)} all-gather(bf16[1024,16]{0,1:T(8,128)(2,1)} %param.19), channel_id=3, replica_groups=mesh['grp'=2,'ep_0'=8,'ep_1'=16,'tp'=2] {'ep_0'}, dimensions={0}, use_global_device_ids=true | all-gather | bytes 294912 | tf_op jit(solution)/shard_map/all_gather | solution.py:72
  61.0 2.3 broadcast_in_dim.43
  63.2 3.7 %all-to-all-start = ((bf16[2,64,8,576]{3,2,1,0:T(8,128)(2,1)}), bf16[2,64,8,576]{3,2,1,0:T(8,128)(2,1)S(1)}, u32[]{:S(2)}, u32[]{:S(2)}) async-start(bf16[2,64,8,576]{3,2,1,0:T(8,128)(2,1)} %broadcast_in_dim.43), calls=%async_computation | async-start | bytes 2621440 | tf_op jit(solution)/shard_map/all_to_all | solution.py:27
  66.9 1.4 copy.90
  69.2 1.1 copy-done.3
  70.2 3.2 fusion
  73.5 3.7 %all_to_all.20 = f32[2,1,1024]{2,1,0:T(1,128)S(1)} all-to-all(f32[2,1,1024]{2,1,0:T(1,128)S(1)} %reshape.137), channel_id=1, replica_groups=mesh['grp'=2,'ep_0'=8,'ep_1'=16,'tp'=2] {'tp'}, dimensions={0} | all-to-all | bytes 16384 | tf_op jit(solution)/shard_map/all_to_all | solution.py:27
  78.6 1.0 convert_reduce_fusion
  79.7 1.1 copy.96
  80.8 2.4 convolution_bitcast_fusion
  83.4 5.9 %all_to_all.21 = f32[2,64,8,513]{3,2,1,0:T(8,128)S(1)} all-to-all(f32[2,64,8,513]{3,2,1,0:T(8,128)S(1)} %maximum_bitcast_fusion), channel_id=1, replica_groups=mesh['grp'=2,'ep_0'=8,'ep_1'=16,'tp'=2] {'tp'}, dimensions={0} | all-to-all | bytes 4202496 | tf_op jit(solution)/shard_map/all_to_all | solution.py:54
  89.3 1.4 reduce_sum.73
  90.6 1.1 slice.14
  92.4 2.2 copy.106
  94.6 1.3 copy.107
  96.3 42.2 %all-gather.5.cloned.1.call-done = bf16[128,8,4,128]{3,1,2,0:T(8,128)(2,1)} async-done(((bf16[8,8,4,128]{3,1,2,0:T(8,128)(2,1)}), bf16[128,8,4,128]{3,1,2,0:T(8,128)(2,1)}) %all-gather.5.cloned.1.call-update) | async-done | bytes 1048592 | tf_op jit(solution)/shard_map/all_gather | solution.py:72
  138.5 1.8 copy.101
  140.7 76.4 %all-gather.7.cloned.1.call-done = bf16[128,1024,16]{1,0,2:T(8,128)(2,1)} async-done(((bf16[8,1024,16]{1,0,2:T(8,128)(2,1)}), bf16[128,1024,16]{1,0,2:T(8,128)(2,1)}) %all-gather.7.cloned.1.call-update) | async-done | bytes 4194320 | tf_op jit(solution)/shard_map/all_gather | solution.py:72
  217.1 4.5 %copy.105 = bf16[8,16,1024,16]{2,3,1,0:T(8,128)(2,1)S(1)} copy(bf16[8,16,1024,16]{2,0,1,3:T(8,128)(2,1)} %bitcast.67) | data formatting | bytes 8388608 | tf_op jit(solution)/shard_map/transpose | solution.py:76
  221.6 1.4 fusion.10
  223.2 4.6 %all_to_all.22 = f32[2,64,2048]{2,1,0:T(8,128)S(1)} all-to-all(f32[2,64,2048]{2,1,0:T(8,128)S(1)} %broadcast_in_dim.79), channel_id=1, replica_groups=mesh['grp'=2,'ep_0'=8,'ep_1'=16,'tp'=2] {'tp'}, dimensions={0} | all-to-all | bytes 2097152 | tf_op jit(solution)/shard_map/all_to_all | solution.py:27
  230.9 119.9 %routed_experts.1 = bf16[64,1024]{1,0:T(8,128)(2,1)} custom-call(f32[16,128]{1,0:T(8,128)} %pad_maximum_fusion.meta_ref, bf16[64,1024]{1,0:T(8,128)(2,1)} %constant_dynamic-slice_fusion.tok_ref, bf16[2048,192]{1,0:T(8,128)(2,1)} %bitcast.65, bf16[2048,192]{1,0:T(8,128)(2,1)} %bitcast.66, bf16[192,2048]{1,0:T(8,128)(2,1)} %bitcast.74), custom_call_target="tpu_custom_call" | custom-call | tf_op jit(solution)/shard_map/routed_experts/pallas_call | solution.py:348
  350.8 1.6 copy.132
  (64 shorter events, 9.0 us)
Async XLA Ops:
  7.2 222.4 %copy-start = (bf16[2048,64]{0,1:T(8,128)(2,1)S(1)}, bf16[2048,64]{0,1:T(8,128)(2,1)}, u32[]{:S(2)}) copy-start(bf16[2048,64]{0,1:T(8,128)(2,1)} %param.21) | copy-start | bytes 786436
  7.2 59.7 %copy-start.4 = (bf16[3,256,576]{1,2,0:T(8,128)(2,1)S(1)}, bf16[3,256,576]{1,2,0:T(8,128)(2,1)}, u32[]{:S(2)}) copy-start(bf16[3,256,576]{1,2,0:T(8,128)(2,1)} %param.14) | copy-start | bytes 2654212
  7.2 131.3 %all-gather.5.cloned.1.call-start = ((), (), s32[]{:S(2)}) async-start(), calls=%async_computation.4 | async-start | bytes 1114112 | tf_op jit(solution)/shard_map/all_gather | solution.py:72
  34.8 182.3 %all-gather.7.cloned.1.call-start = ((), (), s32[]{:S(2)}) async-start(), calls=%async_computation.5 | async-start | bytes 4456448 | tf_op jit(solution)/shard_map/all_gather | solution.py:72
  60.9 7.4 %copy-start.9 = (s32[64]{0:T(128)S(1)}, s32[64]{0:T(128)}, u32[]{:S(2)}) copy-start(s32[64]{0:T(128)} %param.17) | copy-start | bytes 772
  60.9 7.3 %copy-start.10 = (s32[64]{0:T(128)S(1)}, s32[64]{0:T(128)}, u32[]{:S(2)}) copy-start(s32[64]{0:T(128)} %param.16) | copy-start | bytes 772
  63.2 5.9 %all-to-all-start = ((bf16[2,64,8,576]{3,2,1,0:T(8,128)(2,1)}), bf16[2,64,8,576]{3,2,1,0:T(8,128)(2,1)S(1)}, u32[]{:S(2)}, u32[]{:S(2)}) async-start(bf16[2,64,8,576]{3,2,1,0:T(8,128)(2,1)} %broadcast_in_dim.43), calls=%async_computation | async-start | bytes 2621440 | tf_op jit(solution)/shard_map/all_to_all | solution.py:27
  69.2 1.1 copy-start.3
  80.8 2.4 copy-start.2
  90.6 4.0 %copy-start.5 = (bf16[1,2048,192]{1,2,0:T(8,128)(2,1)S(1)}, bf16[1,2048,192]{1,2,0:T(8,128)(2,1)}, u32[]{:S(2)}) copy-start(bf16[1,2048,192]{1,2,0:T(8,128)(2,1)} %param.24) | copy-start | bytes 2359300
  90.6 5.3 %copy-start.7 = (s32[64,6]{0,1:T(8,128)S(1)}, s32[64,6]{0,1:T(8,128)}, u32[]{:S(2)}) copy-start(s32[64,6]{0,1:T(8,128)} %param.22) | copy-start | bytes 4612
  90.6 5.5 %copy-start.1 = (f32[64,8,513]{2,1,0:T(8,128)S(1)}, f32[64,8,513]{2,1,0:T(8,128)}, u32[]{:S(2)}) copy-start(f32[64,8,513]{2,1,0:T(8,128)} %reduce_sum.73) | copy-start | bytes 3151876
  223.0 4.8 %copy-start.6 = (bf16[64,2048]{1,0:T(8,128)(2,1)S(1)}, bf16[64,2048]{1,0:T(8,128)(2,1)}, u32[]{:S(2)}) copy-start(bf16[64,2048]{1,0:T(8,128)(2,1)} %param.15) | copy-start | bytes 786436
  223.0 5.7 %copy-start.8 = (f32[2048]{0:T(1024)S(1)}, f32[2048]{0:T(1024)}, u32[]{:S(2)}) copy-start(f32[2048]{0:T(1024)} %param.20) | copy-start | bytes 24580
Sparse Core Ops, SparseCore 0:
  34.9 103.4 all-gather.4
  140.6 76.4 all-gather.6

commit v2 on v1

--- a/solution.py
+++ b/solution.py
@@ -1,3 +1,5 @@
+import functools
+
 import jax
 import jax.numpy as jnp
 from jax import lax
@@ -6,108 +8,17 @@
 from jax.sharding import Mesh
 from jax.sharding import PartitionSpec as P
 
-LATENT = 512
+
+MESH = pl.DeviceIdType.MESH
 VDIM = 128
-EXPERTS = 64
 TOPK = 6
-GROUPS = 2
 CAP = 8
-PIECES = 128
-MESH = pl.DeviceIdType.MESH
 EP = ("ep_0", "ep_1")
 GRP_EP = ("grp", "ep_0", "ep_1")
 
 
 score_scale = 192.0 ** (-0.5)
 epsilon = 1e-06
-
-
-def from_everyone(value, axis):
-    peers = lax.axis_size(axis)
-    return lax.all_to_all(
-        jnp.broadcast_to(value[None], (peers, *value.shape)), axis, 0, 0, tiled=True
-    )
-
-
-def laid_out(pieces, dim):
-    lengths = list(pieces.shape[1:])
-    lengths[dim] *= pieces.shape[0]
-    return jnp.moveaxis(pieces, 0, dim).reshape(lengths)
-
-
-def collect(value, axis, dim):
-    pieces = from_everyone(value, axis)
-    return laid_out(pieces, dim)
-
-
-def of_everyone(value, axis):
-    return from_everyone(value, axis).max(axis=0)
-
-
-def split_up(value, dim, peers):
-    before, after = (value.shape[:dim], value.shape[dim + 1 :])
-    return jnp.moveaxis(value.reshape(*before, peers, -1, *after), dim, 0)
-
-
-def sent_and_summed(value, axis, dim):
-    peers = lax.axis_size(axis)
-    pieces = lax.all_to_all(split_up(value, dim, peers), axis, 0, 0, tiled=True)
-    return jnp.sum(pieces, axis=0)
-
-
-def sent_together(arrays, axis, dim, along):
-    columns = [a.reshape(*a.shape[:along], -1) for a in arrays]
-    both = jnp.concatenate(columns, axis=along)
-    result, at, outs = (sent_and_summed(both, axis, dim), 0, [])
-    for a, column in zip(arrays, columns):
-        piece = result[..., at : at + column.shape[along]]
-        outs.append(piece.reshape(*piece.shape[:along], *a.shape[along:]))
-        at += column.shape[along]
-    return tuple(outs)
-
-
-def stacked_from(value, axes, order):
-    pieces = value[None]
-    for k in order:
-        pieces = lax.all_gather(pieces, axes[k], axis=0, tiled=True)
-    carried = [lax.axis_size(axes[k]) for k in reversed(order)]
-    pieces = pieces.reshape(*carried, *value.shape)
-    turned = sorted(range(len(order)), key=lambda place: order[len(order) - 1 - place])
-    return pieces.transpose(*turned, *range(len(order), pieces.ndim)).reshape(-1, *value.shape)
-
-
-def whole_of(value, axes, order, dim):
-    return laid_out(stacked_from(value, axes, order), dim)
-
-
-def over_copies(value, axis):
-    everything = from_everyone(value, axis)
-    return jnp.sum(everything, axis=0)
-
-
-def masked_scores(queries, block_rows, token_request, token_visible, offset):
-    per_request = block_rows.shape[1]
-    flat_rows = block_rows.reshape(-1, block_rows.shape[2])
-    scores = (
-        jnp.einsum("thc,kc->thk", queries, flat_rows, preferred_element_type=jnp.float32)
-        * score_scale
-    )
-    column = jnp.arange(flat_rows.shape[0], dtype=jnp.int32)
-    owner_id = column // per_request
-    position = column % per_request + offset
-    allowed = (owner_id[None, :] == token_request[:, None]) & (
-        position[None, :] < token_visible[:, None]
-    )
-    return (jnp.where(allowed[:, None, :], scores, -jnp.inf), flat_rows)
-
-
-def weighted_rows(scores, row_peak, flat_rows):
-    weights = jnp.exp(scores - row_peak[:, :, None]).astype(jnp.bfloat16)
-    totals = jnp.sum(weights.astype(jnp.float32), axis=2)
-    summed = jnp.einsum(
-        "thk,kc->thc", weights, flat_rows[:, :LATENT], preferred_element_type=jnp.float32
-    )
-    return (summed, totals)
 
 
 def ring_ids(axis):
@@ -377,21 +288,302 @@
     )(meta, tokens, gate_weight, up_weight, down_weight)
 
 
-def routing_table(logits, expert_ids):
-    tokens, top = expert_ids.shape
-    experts = jnp.arange(logits.shape[1], dtype=jnp.int32)
-    named = expert_ids[:, :, None] == experts[None, None, :]
-    chosen = jnp.sum(jnp.where(named, logits[:, None, :], 0.0), axis=2)
-    gate_share = jax.nn.softmax(chosen, axis=1).astype(jnp.bfloat16).astype(jnp.float32)
-    counts = jnp.sum(named.astype(jnp.float32), axis=1)
-    token = jnp.arange(tokens, dtype=jnp.int32)
-    before = (token[None, :] < token[:, None]).astype(jnp.float32)
-    earlier = jnp.dot(before, counts, preferred_element_type=jnp.float32)
-    place = jnp.sum(jnp.where(named, earlier[:, None, :], 0.0), axis=2)
-    slot = expert_ids.astype(jnp.float32) * CAP + place
-    fill = jnp.zeros((tokens, 8 - top), jnp.float32)
-    table = jnp.concatenate([slot, fill - 2.0, gate_share, fill], axis=1).T
-    return jnp.concatenate([table, table], axis=1)
+def front_kernel(
+    q_ref, cache_ref, bound_ref, pack_ref, res_ref, gain_ref, router_ref, ids_ref,
+    hidden_ref, normed_ref, meta_ref,
+    buf, cachex, bias, spread, wide, att, attx, full,
+    r_sem, s_sem, c_s, c_r, o_s, o_r,
+):
+    x, x_up, x_down, nx = ring_ids("ep_0")
+    z, z_up, z_down, nz = ring_ids("ep_1")
+    core = lax.axis_index("tp")
+    other = 1 - core
+    toks = res_ref.shape[0]
+    per_half = cache_ref.shape[1]
+    latent = spread.shape[1]
+
+    barrier = pltpu.get_barrier_semaphore()
+    for name, peer in (
+        ("ep_0", x_up), ("ep_0", x_down), ("ep_1", z_up), ("ep_1", z_down), ("tp", other)
+    ):
+        pl.semaphore_signal(barrier, inc=1, device_id={name: peer}, device_id_type=MESH)
+    pl.semaphore_wait(barrier, 5)
+
+    def send(a, xs, zs, axis, up, src=None):
+        if axis == 0:
+            name, peer = "ep_0", (x_up if up else x_down)
+        else:
+            name, peer = "ep_1", (z_up if up else z_down)
+        here = buf.at[a, xs, zs]
+        return pltpu.make_async_remote_copy(
+            src_ref=here if src is None else src,
+            dst_ref=here,
+            send_sem=s_sem.at[a, axis, 0 if up else 1],
+            recv_sem=r_sem.at[a, xs, zs],
+            device_id={name: peer},
+            device_id_type=MESH,
+        )
+
+    def arrived(a, xs, zs):
+        wait_bytes(buf.at[a, xs, zs], r_sem.at[a, xs, zs])
+
+    def at(a, first, second):
+        xs, zs = (first, second) if a == 0 else (second, first)
+        return lax.rem(xs + nx, nx), lax.rem(zs + nz, nz)
+
+    spans = ((nx, nz), (nz, nx))
+    places = ((x, z), (z, x))
+
+    def start_own(a):
+        src = pack_ref.at[a]
+        for axis in (a, 1 - a):
+            for up in (True, False):
+                send(a, x, z, axis, up, src).start()
+
+    def first_ring(a, t):
+        (nf, _), (f, s) = spans[a], places[a]
+        for up in (True, False):
+            last = nf // 2 if up else nf // 2 - 1
+
+            @pl.when((t >= 1) & (t <= last))
+            def _(up=up, last=last):
+                xs, zs = at(a, f - t if up else f + t, s)
+                arrived(a, xs, zs)
+
+                @pl.when(t < last)
+                def _():
+                    send(a, xs, zs, a, up).start()
+
+                send(a, xs, zs, 1 - a, True).start()
+                send(a, xs, zs, 1 - a, False).start()
+
+    def second_ring(a, d, h):
+        (nf, ns), (f, s) = spans[a], places[a]
+        for below in (True, False):
+            if below:
+                held = (d >= 0) & (d <= nf // 2)
+            else:
+                held = (d >= 1) & (d <= nf // 2 - 1)
+            for up in (True, False):
+                last = ns // 2 if up else ns // 2 - 1
+
+                @pl.when(held & (h >= 1) & (h <= last))
+                def _(below=below, up=up, last=last):
+                    xs, zs = at(a, f - d if below else f + d, s - h if up else s + h)
+                    arrived(a, xs, zs)
+
+                    @pl.when(h < last)
+                    def _():
+                        send(a, xs, zs, 1 - a, up).start()
+
+    start_own(0)
+    start_own(1)
+    swap = pltpu.make_async_remote_copy(
+        src_ref=cache_ref, dst_ref=cachex, send_sem=c_s, recv_sem=c_r,
+        device_id={"tp": other}, device_id_type=MESH,
+    )
+    swap.start()
+    for a in range(2):
+        buf[a, x, z] = pack_ref[a]
+
+    keys_n = bias.shape[2]
+    column = lax.broadcasted_iota(jnp.int32, (toks, keys_n), 1)
+    owner = column // per_half
+    place = column % per_half
+    limit = jnp.zeros((toks, keys_n), jnp.int32)
+    for r in range(cache_ref.shape[0]):
+        limit = jnp.where(owner == r, bound_ref[:, r : r + 1], limit)
+    for half, index in ((0, core), (1, other)):
+        bias[half] = jnp.where(place + index * per_half < limit, 0.0, -jnp.inf)
+    source = lax.broadcasted_iota(jnp.int32, (latent, 2 * latent), 0)
+    target = lax.broadcasted_iota(jnp.int32, (latent, 2 * latent), 1)
+    for group in range(2):
+        goal = (source // 4) * 8 + group * 4 + source % 4
+        spread[group] = jnp.where(goal == target, 1.0, 0.0).astype(jnp.bfloat16)
+
+    expert_n = router_ref.shape[1]
+    experts = lax.broadcasted_iota(jnp.int32, (toks, expert_n), 1)
+    named = [experts == ids_ref[:, k : k + 1] for k in range(TOPK)]
+
+    def attend(p):
+        queries = q_ref[pl.ds(2 * p, 2)].reshape(2 * toks, q_ref.shape[2])
+
+        def scored(ref, half):
+            keys = ref[...].reshape(keys_n, ref.shape[2])
+            scores = lax.dot_general(
+                queries, keys, (((1,), (1,)), ((), ())), preferred_element_type=jnp.float32
+            )
+            both = scores.reshape(2, toks, keys_n) * score_scale + bias[half][None]
+            return both.reshape(2 * toks, keys_n)
+
+        near = scored(cache_ref, 0)
+        far = scored(cachex, 1)
+        peak = jnp.maximum(
+            jnp.max(near, axis=1, keepdims=True), jnp.max(far, axis=1, keepdims=True)
+        )
+        near = jnp.exp(near - peak).astype(jnp.bfloat16)
+        far = jnp.exp(far - peak).astype(jnp.bfloat16)
+        totals = jnp.sum(near.astype(jnp.float32), axis=1, keepdims=True) + jnp.sum(
+            far.astype(jnp.float32), axis=1, keepdims=True
+        )
+
+        def summed(weights, ref):
+            rows = ref[:, :, :latent].reshape(keys_n, latent)
+            return jnp.dot(weights, rows, preferred_element_type=jnp.float32)
+
+        context = ((summed(near, cache_ref) + summed(far, cachex)) / totals).astype(jnp.bfloat16)
+        wide[p] = jnp.dot(
+            context, spread[p % 2], preferred_element_type=jnp.float32
+        ).astype(jnp.bfloat16)
+
+    pieces = q_ref.shape[0] // 2
+    ticks = nx // 2 + nz // 2 + 1
+
+    def tick(t, carry):
+        for a in range(2):
+            first_ring(a, t)
+        for d in range(nx // 2 + 1):
+            second_ring(0, d, t - d)
+        for h in range(1, nx // 2 + 1):
+            second_ring(1, t - h, h)
+
+        @pl.when((t >= 1) & (t <= pieces))
+        def _():
+            attend(t - 1)
+
+        return carry
+
+    swap.wait_recv()
+    lax.fori_loop(0, ticks, tick, 0)
+    for p in range(max(ticks - 1, 0), pieces):
+        attend(p)
+
+    columns = nx * nz * 16
+    part = jnp.zeros((toks, columns), jnp.float32)
+    for a in range(2):
+        values = buf[a, :, :, 32:40, :].reshape(2 * latent, buf.shape[4])
+        by_side = []
+        for b in range(2):
+            stacked = jnp.concatenate(
+                [wide[2 * a + g, b * toks : (b + 1) * toks, :] for g in range(2)], axis=0
+            )
+            by_side.append(
+                jnp.dot(
+                    stacked, values[:, b * VDIM : (b + 1) * VDIM],
+                    preferred_element_type=jnp.float32,
+                ).astype(jnp.bfloat16)
+            )
+        for g in range(2):
+            heads = jnp.concatenate(
+                [side[g * toks : (g + 1) * toks] for side in by_side], axis=1
+            )
+            weights = buf[a, :, :, g * 16 : (g + 1) * 16, :].reshape(columns, buf.shape[4])
+            part = part + lax.dot_general(
+                heads, weights, (((1,), (1,)), ((), ())), preferred_element_type=jnp.float32
+            )
+    att[...] = part
+    merge = pltpu.make_async_remote_copy(
+        src_ref=att, dst_ref=attx, send_sem=o_s, recv_sem=o_r,
+        device_id={"tp": other}, device_id_type=MESH,
+    )
+    merge.start()
+
+    counts = jnp.zeros((toks, expert_n), jnp.float32)
+    for hit in named:
+        counts = counts + jnp.where(hit, 1.0, 0.0)
+    token_a = lax.broadcasted_iota(jnp.int32, (toks, toks), 0)
+    token_b = lax.broadcasted_iota(jnp.int32, (toks, toks), 1)
+    before = jnp.where(token_b < token_a, 1.0, 0.0).astype(jnp.bfloat16)
+    earlier = jnp.dot(before, counts.astype(jnp.bfloat16), preferred_element_type=jnp.float32)
+    lane = lax.broadcasted_iota(jnp.int32, (toks, 128), 1)
+    table = jnp.zeros((toks, 128), jnp.float32)
+    for k, hit in enumerate(named):
+        spot = jnp.sum(jnp.where(hit, earlier, 0.0), axis=1, keepdims=True)
+        slot = ids_ref[:, k : k + 1].astype(jnp.float32) * CAP + spot
+        table = jnp.where(lane == k, slot, table)
+
+    merge.wait_recv()
+    hidden = (res_ref[...].astype(jnp.float32) + (att[...] + attx[...])).astype(jnp.bfloat16)
+    hidden_wide = hidden.astype(jnp.float32)
+    square = jnp.mean(hidden_wide * hidden_wide, axis=1, keepdims=True)
+    normed = (hidden_wide * lax.rsqrt(square + epsilon) * gain_ref[...]).astype(jnp.bfloat16)
+    logits = jnp.dot(normed, router_ref[...], preferred_element_type=jnp.float32)
+    chosen = [
+        jnp.sum(jnp.where(hit, logits, 0.0), axis=1, keepdims=True) for hit in named
+    ]
+    top = functools.reduce(jnp.maximum, chosen)
+    raised = [jnp.exp(value - top) for value in chosen]
+    total = functools.reduce(jnp.add, raised)
+    for k, value in enumerate(raised):
+        share = (value / total).astype(jnp.bfloat16).astype(jnp.float32)
+        table = jnp.where(lane == 8 + k, share, table)
+    meta_ref[...] = jnp.concatenate([table, table], axis=0).T[:16]
+    half_width = normed_ref.shape[1]
+    mine = pl.ds(pl.multiple_of(core * half_width, half_width), half_width)
+    full[0] = hidden
+    full[1] = normed
+    hidden_ref[...] = full[0, :, mine]
+    normed_ref[...] = full[1, :, mine]
+
+    swap.wait_send()
+    merge.wait_send()
+    for a in range(2):
+        nf, ns = spans[a]
+        for up in (0, 1):
+            if a == 0:
+                wait_bytes(buf.at[0, pl.ds(0, nf // 2 - up), 0], s_sem.at[0, 0, up])
+                wait_bytes(buf.at[0, :, pl.ds(0, ns // 2 - up)], s_sem.at[0, 1, up])
+            else:
+                wait_bytes(buf.at[1, 0, pl.ds(0, nf // 2 - up)], s_sem.at[1, 1, up])
+                wait_bytes(buf.at[1, pl.ds(0, ns // 2 - up)], s_sem.at[1, 0, up])
+
+
+def attention_front(
+    queries, latent_cache, residual, token_request, token_visible,
+    value_proj, out_proj, norm_gain, router, expert_ids,
+):
+    nx, nz = lax.axis_size("ep_0"), lax.axis_size("ep_1")
+    toks, heads, width = queries.shape
+    requests, per_half, _ = latent_cache.shape
+    model = residual.shape[1]
+    latent = value_proj.shape[1] * nx * nz
+    bf, f32 = jnp.bfloat16, jnp.float32
+    quarter = heads // 4 * VDIM
+    out_rows = out_proj.reshape(4, quarter, -1).transpose(0, 2, 1).reshape(2, 32, quarter)
+    value_rows = value_proj.reshape(2, 2, 2, 4, VDIM).transpose(0, 1, 3, 2, 4)
+    pack = jnp.concatenate([out_rows, value_rows.reshape(2, 8, quarter)], axis=1)
+    request = jnp.arange(requests, dtype=jnp.int32)
+    bound = jnp.where(token_request[:, None] == request, token_visible[:, None], 0)
+    dma = pltpu.SemaphoreType.DMA
+    half = model // lax.axis_size("tp")
+    return pl.pallas_call(
+        front_kernel,
+        out_shape=(
+            jax.ShapeDtypeStruct((toks, half), bf),
+            jax.ShapeDtypeStruct((toks, half), bf),
+            jax.ShapeDtypeStruct((16, 2 * toks), f32),
+        ),
+        in_specs=[pl.BlockSpec(memory_space=pltpu.VMEM)] * 8,
+        out_specs=(pl.BlockSpec(memory_space=pltpu.VMEM),) * 3,
+        scratch_shapes=[
+            pltpu.VMEM((2, nx, nz, 40, quarter), bf),
+            pltpu.VMEM(latent_cache.shape, bf),
+            pltpu.VMEM((2, toks, requests * per_half), f32),
+            pltpu.VMEM((2, latent, 2 * latent), bf),
+            pltpu.VMEM((heads // 2, 2 * toks, 2 * latent), bf),
+            pltpu.VMEM((toks, model), f32),
+            pltpu.VMEM((toks, model), f32),
+            pltpu.VMEM((2, toks, model), bf),
+            dma((2, nx, nz)), dma((2, 2, 2)), dma, dma, dma, dma,
+        ],
+        compiler_params=pltpu.CompilerParams(
+            collective_id=2, has_side_effects=True, vmem_limit_bytes=60 * 2**20
+        ),
+        name="attention_front",
+    )(
+        queries.transpose(1, 0, 2), latent_cache, bound, pack, residual,
+        norm_gain.reshape(1, model), router, expert_ids,
+    )
 
 
 def body(
@@ -409,42 +601,13 @@
     up_weight,
     down_weight,
 ):
-    all_heads = collect(queries, "tp", 1)
-    offset = lax.axis_index("tp") * latent_cache.shape[1]
-    scores, flat_rows = masked_scores(all_heads, latent_cache, token_request, token_visible, offset)
-    row_peak = of_everyone(jnp.max(scores, axis=2), "tp")
-    part_sum, part_total = weighted_rows(scores, row_peak, flat_rows)
-    summed, totals = sent_together((part_sum, part_total), "tp", 1, 2)
-    context = (summed / totals[:, :, None]).astype(jnp.bfloat16)
-    tokens_here = context.shape[0]
-    heads_here = context.shape[1]
-    head_values = jnp.einsum(
-        "thl,hlv->thv",
-        context,
-        whole_of(value_proj, EP, (0, 1), 1),
-        preferred_element_type=jnp.float32,
+    hidden_part, normed_part, meta = attention_front(
+        queries, latent_cache, residual, token_request, token_visible,
+        value_proj, out_proj, norm_gain, router, expert_ids,
     )
-    heads_out = head_values.astype(jnp.bfloat16).reshape(tokens_here, heads_here * VDIM)
-    attention_part = jnp.dot(
-        heads_out, whole_of(out_proj, EP, (0, 1), 1), preferred_element_type=jnp.float32
+    expert_out = routed_experts(
+        meta, normed_part, gate_weight[0], up_weight[0], down_weight[0]
     )
-    attention = over_copies(attention_part, "tp")
-    hidden = (residual.astype(jnp.float32) + attention).astype(jnp.bfloat16)
-    hidden_wide = hidden.astype(jnp.float32)
-    normed = (
-        hidden_wide
-        * lax.rsqrt(jnp.mean(hidden_wide * hidden_wide, axis=1, keepdims=True) + epsilon)
-        * norm_gain
-    ).astype(jnp.bfloat16)
-    logits = jnp.dot(normed, router, preferred_element_type=jnp.float32)
-    meta = routing_table(logits, expert_ids)
-    half_width = normed.shape[1] // lax.axis_size("tp")
-    core_start = lax.axis_index("tp") * half_width
-    normed_share = lax.dynamic_slice_in_dim(normed, core_start, half_width, 1)
-    expert_out = routed_experts(
-        meta, normed_share, gate_weight[0], up_weight[0], down_weight[0]
-    )
-    hidden_part = lax.dynamic_slice_in_dim(hidden, core_start, half_width, 1)
     return (hidden_part, expert_out)
 
 

time: 360 us -> 231 us (0.64)
  waiting for transfers between devices: 119 us -> 0 us
  Pallas kernels: 120 us -> 218 us
  blocking collectives: 66.1 us -> 0 us
  between operations: 14.3 us -> 0.7 us
  local copies, waits for them, and re-layouts: 22.8 us -> 10.5 us
  matrix products: 7.74 us -> 0 us
  starting transfers between devices: 3.78 us -> 0 us
    all_gather x2 -> x0, waiting for transfers between devices: 119 us -> none  [stacked_from(): pieces = lax.all_gather(pieces, axes[k], axis=0, tiled=True)]
    pallas_call x0 -> x1, Pallas kernels: none -> 98.5 us  [attention_front(): pl.pallas_call(front_kernel, out_shape=(jax.ShapeDtypeStruct((toks, half)...]
    all_gather x2 -> x0, blocking collectives: 52 us -> none  [stacked_from(): pieces = lax.all_gather(pieces, axes[k], axis=0, tiled=True)]
    all_to_all x3 -> x0, blocking collectives: 14.2 us -> none  [the longest x2 8.32 us: from_everyone(): lax.all_to_all(jnp.broadcast_to(value[None], (peers, *value.shape)), axis...]
    dot_general x6 -> x0, matrix products: 7.74 us -> none  [the longest x1 3.15 us: masked_scores(): jnp.einsum('thc,kc->thk', queries, flat_rows, preferred_element_type=jnp....]
    transpose x2 -> x0, local copies, waits for them, and re-layouts: 6.31 us -> none  [stacked_from(): pieces.transpose(*turned, *range(len(order), pieces.ndim))]
    all_to_all x1 -> x0, starting transfers between devices: 3.65 us -> none  [from_everyone(): lax.all_to_all(jnp.broadcast_to(value[None], (peers, *value.shape)), axis...]
    unnamed x30 -> x22, local copies, waits for them, and re-layouts: 8.65 us -> 8.93 us
  transfers between devices with their start and end apart: 3 -> 0, of which waited for: 3 -> 0; matrix products, arithmetic and copies ran while one was open for 6% -> 0% of each run, Pallas kernels for 0% -> 0%
where the time goes in v2:
time: 231 us
  Pallas kernels  218 us (94%)
  local copies, waits for them, and re-layouts  10.5 us (5%)
    pallas_call x1, Pallas kernels, routed_experts(): pl.pallas_call(moe_kernel, out_shape=jax.ShapeDtypeStruct((toks, half), b...  119 us
    pallas_call x1, Pallas kernels, attention_front(): pl.pallas_call(front_kernel, out_shape=(jax.ShapeDtypeStruct((toks, half)...  98.5 us
    unnamed x22, local copies, waits for them, and re-layouts  8.93 us

profile of v2, /device:TPU:80, one launch (start us, length us, event | category | flops | bytes accessed | tf_op | source)
XLA Modules:
  0.0 230.8 jit_solution(2418197757511151913)
XLA Ops:
  0.6 0.0 copy-start.5
  0.6 0.0 copy-start.3
  0.6 0.8 copy.29
  1.4 1.4 fusion.bound_ref
  2.8 0.8 copy.28
  3.6 0.6 pad_maximum_fusion.pack_ref
  4.2 1.4 copy.20.ids_ref
  5.6 0.0 copy-done.5
  5.6 1.0 copy.19.router_ref
  6.6 0.0 copy-done.3
  6.6 0.9 copy.27
  7.5 0.0 copy-done
  7.5 1.4 copy.18.cache_ref
  8.9 98.5 %attention_front.1 = (bf16[64,1024]{1,0:T(8,128)(2,1)}, bf16[64,1024]{1,0:T(8,128)(2,1)}, f32[16,128]{1,0:T(8,128)}) custom-call(bf16[8,64,576]{2,1,0:T(8,128)(2,1)} %bitcast.20, bf16[3,256,576]{2,1,0:T(8,128)(2,1)} %copy.18.cache_ref, s32[64,3]{1,0:T(8,128)} %fusion.bound_ref, bf16[2,40,256]{2,1,0:T(8,128)(2,1)} %pad_maximum_fusion.pack_ref, ...), custom_call_target="tpu_custom_call" | custom-call | tf_op jit(solution)/shard_map/attention_front/pallas_call | solution.py:559
  107.5 0.0 copy-done.1
  107.5 0.0 copy-start.2
  107.5 1.3 copy.21
  108.8 0.0 copy-done.2
  108.8 1.3 copy.22
  110.1 119.1 %routed_experts.1 = bf16[64,1024]{1,0:T(8,128)(2,1)} custom-call(f32[16,128]{1,0:T(8,128)} %get-tuple-element.6.meta_ref, bf16[64,1024]{1,0:T(8,128)(2,1)} %get-tuple-element.7.tok_ref, bf16[2048,192]{1,0:T(8,128)(2,1)} %bitcast.18, bf16[2048,192]{1,0:T(8,128)(2,1)} %bitcast.19, bf16[192,2048]{1,0:T(8,128)(2,1)} %bitcast.21), custom_call_target="tpu_custom_call" | custom-call | tf_op jit(solution)/shard_map/routed_experts/pallas_call | solution.py:259
  229.2 0.0 copy-done.6
  229.2 0.7 copy.32
  229.9 0.3 copy-done.4
  230.2 0.7 copy.33
  (5 shorter events, 0.0 us)
Async XLA Ops:
  0.6 5.0 %copy-start.5 = (bf16[2048,64]{0,1:T(8,128)(2,1)S(1)}, bf16[2048,64]{0,1:T(8,128)(2,1)}, u32[]{:S(2)}) copy-start(bf16[2048,64]{0,1:T(8,128)(2,1)} %param.21) | copy-start | bytes 786436
  0.6 6.0 %copy-start.3 = (bf16[64,8,576]{2,1,0:T(8,128)(2,1)S(1)}, bf16[64,8,576]{2,1,0:T(8,128)(2,1)}, u32[]{:S(2)}) copy-start(bf16[64,8,576]{2,1,0:T(8,128)(2,1)} %param.13) | copy-start | bytes 1769476
  5.6 1.9 copy-start
  8.9 98.6 %copy-start.1 = (bf16[1,2048,192]{1,2,0:T(8,128)(2,1)S(1)}, bf16[1,2048,192]{1,2,0:T(8,128)(2,1)}, u32[]{:S(2)}) copy-start(bf16[1,2048,192]{1,2,0:T(8,128)(2,1)} %param.23) | copy-start | bytes 2359300
  107.5 1.3 copy-start.2
  110.1 119.1 %copy-start.6 = (bf16[64,1024]{1,0:T(8,128)(2,1)S(1)}, bf16[64,1024]{1,0:T(8,128)(2,1)}, u32[]{:S(2)}) copy-start(bf16[64,1024]{1,0:T(8,128)(2,1)} %get-tuple-element.10) | copy-start | bytes 393220
  229.2 1.0 copy-start.4
